TPU v7x, 32 devices: a whole 2x2x4 slice. The times are simulated.
32 devices in a mesh: row: 8 (over y, x, core), col: 4 (over z).
Axes of the slice: x: 2, y: 2, z: 4, core: 2. Of those that a mesh axis runs over, the one named last changes fastest.
Arguments:
- pair_factors: float32 [12288, 1024], P(('row', 'col')), may hold values from -0.09375 to 0.09375
- k_prev: float32 [12288, 12288], P('row', 'col'), as said below
- energies: float32 [12288], P('row'), may hold values from 0.3 to 2
Outputs:
- casida: float32 [12288, 12288], P('row', 'col')
- vectors: float32 [12288, 8], P('row')
- images: float32 [12288, 8], P('row')
- tridiagonal: float32 [2, 8], replicated
Inputs may be any that keep to these rules, and one draw needn't show every extreme that they name: k_prev is exactly symmetric.
All inputs are finite; a program needn't handle non-finite values.
Results may differ from a plain program's by a relative error of at most 0.0003.
Values sent between devices are 32-bit elements; how exact they have to be, the bound alone decides.
No kernel may reach another device: no remote copies, remote signals or barrier semaphores. Data moves between devices by JAX's collectives and lax.ppermute only.
A program may use at most 128 MiB of HBM per device.

v0:
```python
import jax
import jax.numpy as jnp
from jax import lax
from jax.sharding import PartitionSpec as P

N = 12288
PANEL_W = 512
PC = 8


def from_root(value, axis, root):
    mine = lax.axis_index(axis) == root
    return lax.psum(jnp.where(mine, value, jnp.zeros_like(value)), axis)


def shards(pair_factors, k_prev, energies):
    rows_here, cols_here = k_prev.shape
    per_col = lax.axis_size("row") // lax.axis_size("col")
    row_index = lax.axis_index("row")
    col_index = lax.axis_index("col")
    total = jnp.zeros((rows_here, cols_here), jnp.float32)
    aux_here = pair_factors.shape[1]
    width = PANEL_W
    for start_at in range(0, aux_here, width):
        stop_at = min(start_at + width, aux_here)
        piece = pair_factors[:, start_at:stop_at]
        left_rows = lax.all_gather(piece, "col", axis=0, tiled=True)
        right_parts = []
        for offset in range(per_col):
            right_parts.append(from_root(left_rows, "row", per_col * col_index + offset))
        right_rows = jnp.concatenate(right_parts, axis=0)
        total = total + lax.dot_general(
            left_rows,
            right_rows,
            (((1,), (1,)), ((), ())),
            precision=lax.Precision.HIGHEST,
            preferred_element_type=jnp.float32,
        )
    global_rows = row_index * rows_here + jnp.arange(rows_here, dtype=jnp.int32)
    global_cols = col_index * cols_here + jnp.arange(cols_here, dtype=jnp.int32)
    on_diagonal = global_rows[:, None] == global_cols[None, :]
    casida = 4.0 * (k_prev + total) + jnp.where(on_diagonal, energies[:, None], 0.0)
    col_ids = jnp.arange(PC, dtype=jnp.int32)
    scale = jnp.sqrt(jnp.float32(N))
    diag_list = []
    sub_list = []
    spread = from_root(casida[:, :PC], "col", 0)
    panel = lax.all_gather(spread, "row", axis=0, tiled=True)
    total_rows = panel.shape[0]
    all_rows = jnp.arange(total_rows, dtype=jnp.int32)
    upper_full = jnp.zeros((total_rows, PC), jnp.float32)
    lower_full = jnp.zeros((total_rows, PC), jnp.float32)
    for column_at in range(PC):
        column = (
            panel[:, column_at]
            - jnp.dot(upper_full, lower_full[column_at], precision=lax.Precision.HIGHEST)
            - jnp.dot(lower_full, upper_full[column_at], precision=lax.Precision.HIGHEST)
        )
        diag_list.append(column[column_at])
        below = jnp.where(all_rows > column_at, column, 0.0)
        lead = column[column_at + 1]
        sigma = jnp.sum(below * below)
        root = jnp.sqrt(sigma)
        alpha = jnp.where(lead >= 0, -root, root)
        length = jnp.sqrt(jnp.maximum(2.0 * (sigma + jnp.abs(lead) * root), 1.0))
        unit = (below - alpha * (all_rows == column_at + 1).astype(jnp.float32)) / length
        unit_cols = lax.dynamic_slice_in_dim(unit, col_index * cols_here, cols_here, 0)
        partial_rows = jnp.dot(casida, unit_cols, precision=lax.Precision.HIGHEST)
        placed = lax.dynamic_update_slice_in_dim(
            jnp.zeros((total_rows,), jnp.float32), partial_rows, row_index * rows_here, 0
        )
        image = lax.psum(placed, ("row", "col"))
        image = image - jnp.dot(
            upper_full,
            jnp.dot(lower_full.T, unit, precision=lax.Precision.HIGHEST),
            precision=lax.Precision.HIGHEST,
        )
        image = image - jnp.dot(
            lower_full,
            jnp.dot(upper_full.T, unit, precision=lax.Precision.HIGHEST),
            precision=lax.Precision.HIGHEST,
        )
        image = 2.0 * image
        partner = image - jnp.sum(image * unit) * unit
        pick = (col_ids == column_at).astype(jnp.float32)[None, :]
        upper_full = upper_full + unit[:, None] * pick
        lower_full = lower_full + partner[:, None] * pick
        sub_list.append(alpha)
    upper = lax.dynamic_slice_in_dim(upper_full, row_index * rows_here, rows_here, 0)
    lower = lax.dynamic_slice_in_dim(lower_full, row_index * rows_here, rows_here, 0)
    tridiagonal = jnp.stack([jnp.stack(diag_list), jnp.stack(sub_list)])
    return (casida, scale * upper, scale * lower, tridiagonal)


def solution(mesh):
    in_specs = (P(("row", "col"), None), P("row", "col"), P("row"))
    out_specs = (P("row", "col"), P("row", None), P("row", None), P())
    return jax.shard_map(shards, mesh=mesh, in_specs=in_specs, out_specs=out_specs, check_vma=False)
```

profile of v0, /device:TPU:0, one launch (start us, length us, event | category | flops | bytes accessed | tf_op | source)
XLA Modules:
  0.0 965.6 jit_solution(18281307544850483089)
XLA Ops:
  10.7 65.6 %all-gather.5.cloned.1.call-done = f32[1536,512]{1,0:T(8,128)} async-done(((f32[384,512]{1,0:T(8,128)}), f32[1536,512]{1,0:T(8,128)}) %all-gather.5.cloned.1.call-update) | async-done | bytes 3145744 | tf_op jit(solution)/shard_map/all_gather | solution.py:27
  81.9 58.1 %all-gather.3.cloned.1.call-done = f32[1536,512]{1,0:T(8,128)} async-done(((f32[384,512]{1,0:T(8,128)}), f32[1536,512]{1,0:T(8,128)}) %all-gather.3.cloned.1.call-update) | async-done | bytes 3145744 | tf_op jit(solution)/shard_map/all_gather | solution.py:27
  146.3 18.8 %copy.9 = f32[1536,3072]{0,1:T(8,128)} copy(f32[1536,3072]{1,0:T(8,128)} %param.4) | data formatting | bytes 37748736 | tf_op args[1]
  165.1 151.2 %all-reduce.3.cloned.1.call-done = (f32[1536,512]{1,0:T(8,128)}, f32[1536,512]{1,0:T(8,128)}, f32[1536,512]{1,0:T(8,128)}, f32[1536,512]{1,0:T(8,128)}) async-done(((f32[1536,512]{1,0:T(8,128)}, f32[1536,512]{1,0:T(8,128)}, f32[1536,512]{1,0:T(8,128)}, f32[1536,512]{1,0:T(8,128)}), (f32[1536,512]{1,0:T(8,128)}, f32[1536,512]{1,0:T(8,128)}, f32[1536,512]{1,0:T(8,128)}, ...) | async-done | bytes 12582928 | tf_op jit(solution)/shard_map/psum | solution.py:13
  316.4 34.6 %fusion.2 = f32[3072,1536]{1,0:T(8,128)} fusion(f32[1536,512]{1,0:T(8,128)S(1)} %copy-done.1, f32[1536,512]{1,0:T(8,128)} %get-tuple-element.12, f32[1536,512]{1,0:T(8,128)} %get-tuple-element.13), kind=kOutput, calls=%fused_computation.3 | convolution fusion | flops 28992602112 | bytes 28311552 | tf_op jit(solution)/shard_map/dot_general | solution.py:32
  351.0 39.2 %fusion.1 = f32[1536,3072]{0,1:T(8,128)S(1)} fusion(f32[1536,3072]{0,1:T(8,128)} %copy.9, f32[3072,1536]{1,0:T(8,128)} %fusion.2, f32[1536,512]{1,0:T(8,128)} %all-gather.5.cloned.1.call-done, f32[1536]{0:T(1024)S(1)} %copy-done.2, s32[1536]{0:T(1024)S(1)} %iota_add_fusion.1, s32[3072]{0:T(1024)S(1)} %iota_add_fusion, f32[1536,512]{1,0:T(8,128)} %get-tuple-element.14, ...), kind=kOutput, calls=%fused_computation.2 | convolution fusion | flops 29020913664 | bytes 66084864 | tf_op jit(solution)/shard_map/dot_general | solution.py:32
  396.7 19.5 %psum.95 = f32[1536,8]{0,1:T(8,128)S(1)} all-reduce(f32[1536,8]{0,1:T(8,128)S(1)} %slice_select_fusion), channel_id=1, replica_groups=mesh['row'=8,'col'=4] {'col'}, use_global_device_ids=true, to_apply=%region_4.5 | all-reduce | flops 12288 | bytes 98304 | tf_op jit(solution)/shard_map/psum | solution.py:13
  430.6 12.9 %convolution_reduce_fusion.7 = f32[1536]{0:T(1024)S(1)} fusion(f32[1536,3072]{0,1:T(8,128)} %copy-done, f32[3072,1]{0,1:T(1,128)S(1)} %bitcast.304), kind=kOutput, calls=%fused_computation.21 | convolution fusion | flops 56623104 | bytes 18892800 | tf_op jit(solution)/shard_map/dot_general | solution.py:68
  443.8 38.0 %psum.96 = f32[12288]{0:T(1024)S(1)} all-reduce(f32[12288]{0:T(1024)S(1)} %dynamic_update_slice.24), channel_id=1, replica_groups=mesh['row'=8,'col'=4] {'row','col'}, use_global_device_ids=true, to_apply=%region_6.7 | all-reduce | flops 12288 | bytes 98304 | tf_op jit(solution)/shard_map/psum | solution.py:72
  493.4 12.9 %convolution_reduce_fusion.6 = f32[1536]{0:T(1024)S(1)} fusion(f32[1536,3072]{0,1:T(8,128)} %copy-done, f32[3072,1]{0,1:T(1,128)S(1)} %bitcast.298), kind=kOutput, calls=%fused_computation.20 | convolution fusion | flops 56623104 | bytes 18892800 | tf_op jit(solution)/shard_map/dot_general | solution.py:68
  506.6 41.5 %psum.97 = f32[12288]{0:T(1024)S(1)} all-reduce(f32[12288]{0:T(1024)S(1)} %dynamic_update_slice.25), channel_id=1, replica_groups=mesh['row'=8,'col'=4] {'row','col'}, use_global_device_ids=true, to_apply=%region_9.10 | all-reduce | flops 12288 | bytes 98304 | tf_op jit(solution)/shard_map/psum | solution.py:72
  558.1 12.9 %convolution_reduce_fusion.5 = f32[1536]{0:T(1024)S(1)} fusion(f32[1536,3072]{0,1:T(8,128)} %copy-done, f32[3072,1]{0,1:T(1,128)S(1)} %bitcast.299), kind=kOutput, calls=%fused_computation.19 | convolution fusion | flops 56623104 | bytes 18892800 | tf_op jit(solution)/shard_map/dot_general | solution.py:68
  571.3 39.9 %psum.98 = f32[12288]{0:T(1024)S(1)} all-reduce(f32[12288]{0:T(1024)S(1)} %dynamic_update_slice.26), channel_id=1, replica_groups=mesh['row'=8,'col'=4] {'row','col'}, use_global_device_ids=true, to_apply=%region_12.13 | all-reduce | flops 12288 | bytes 98304 | tf_op jit(solution)/shard_map/psum | solution.py:72
  621.3 12.9 %convolution_reduce_fusion.4 = f32[1536]{0:T(1024)S(1)} fusion(f32[1536,3072]{0,1:T(8,128)} %copy-done, f32[3072,1]{0,1:T(1,128)S(1)} %bitcast.300), kind=kOutput, calls=%fused_computation.18 | convolution fusion | flops 56623104 | bytes 18892800 | tf_op jit(solution)/shard_map/dot_general | solution.py:68
  634.5 41.6 %psum.99 = f32[12288]{0:T(1024)S(1)} all-reduce(f32[12288]{0:T(1024)S(1)} %dynamic_update_slice.27), channel_id=1, replica_groups=mesh['row'=8,'col'=4] {'row','col'}, use_global_device_ids=true, to_apply=%region_15.16 | all-reduce | flops 12288 | bytes 98304 | tf_op jit(solution)/shard_map/psum | solution.py:72
  686.5 12.9 %convolution_reduce_fusion.3 = f32[1536]{0:T(1024)S(1)} fusion(f32[1536,3072]{0,1:T(8,128)} %copy-done, f32[3072,1]{0,1:T(1,128)S(1)} %bitcast.301), kind=kOutput, calls=%fused_computation.17 | convolution fusion | flops 56623104 | bytes 18892800 | tf_op jit(solution)/shard_map/dot_general | solution.py:68
  699.7 40.0 %psum.100 = f32[12288]{0:T(1024)S(1)} all-reduce(f32[12288]{0:T(1024)S(1)} %dynamic_update_slice.28), channel_id=1, replica_groups=mesh['row'=8,'col'=4] {'row','col'}, use_global_device_ids=true, to_apply=%region_18.19 | all-reduce | flops 12288 | bytes 98304 | tf_op jit(solution)/shard_map/psum | solution.py:72
  750.0 12.9 %convolution_reduce_fusion.2 = f32[1536]{0:T(1024)S(1)} fusion(f32[1536,3072]{0,1:T(8,128)} %copy-done, f32[3072,1]{0,1:T(1,128)S(1)} %bitcast.302), kind=kOutput, calls=%fused_computation.16 | convolution fusion | flops 56623104 | bytes 18892800 | tf_op jit(solution)/shard_map/dot_general | solution.py:68
  763.3 41.2 %psum.101 = f32[12288]{0:T(1024)S(1)} all-reduce(f32[12288]{0:T(1024)S(1)} %dynamic_update_slice.29), channel_id=1, replica_groups=mesh['row'=8,'col'=4] {'row','col'}, use_global_device_ids=true, to_apply=%region_21.22 | all-reduce | flops 12288 | bytes 98304 | tf_op jit(solution)/shard_map/psum | solution.py:72
  814.5 12.9 %convolution_reduce_fusion.1 = f32[1536]{0:T(1024)S(1)} fusion(f32[1536,3072]{0,1:T(8,128)} %copy-done, f32[3072,1]{0,1:T(1,128)S(1)} %bitcast.303), kind=kOutput, calls=%fused_computation.15 | convolution fusion | flops 56623104 | bytes 18892800 | tf_op jit(solution)/shard_map/dot_general | solution.py:68
  827.7 40.0 %psum.102 = f32[12288]{0:T(1024)S(1)} all-reduce(f32[12288]{0:T(1024)S(1)} %dynamic_update_slice.30), channel_id=1, replica_groups=mesh['row'=8,'col'=4] {'row','col'}, use_global_device_ids=true, to_apply=%region_24.25 | all-reduce | flops 12288 | bytes 98304 | tf_op jit(solution)/shard_map/psum | solution.py:72
  877.0 18.6 %copy.10 = f32[1536,3072]{1,0:T(8,128)} copy(f32[1536,3072]{0,1:T(8,128)} %copy-done) | data formatting | bytes 37748736
  896.1 12.9 %convolution_reduce_fusion = f32[1536]{0:T(1024)S(1)} fusion(f32[1536,3072]{0,1:T(8,128)} %copy-done, f32[3072,1]{0,1:T(1,128)S(1)} %bitcast.297), kind=kOutput, calls=%fused_computation.14 | convolution fusion | flops 56623104 | bytes 18892800 | tf_op jit(solution)/shard_map/dot_general | solution.py:68
  909.3 41.0 %psum.103 = f32[12288]{0:T(1024)S(1)} all-reduce(f32[12288]{0:T(1024)S(1)} %dynamic_update_slice.31), channel_id=1, replica_groups=mesh['row'=8,'col'=4] {'row','col'}, use_global_device_ids=true, to_apply=%region_27.28 | all-reduce | flops 12288 | bytes 98304 | tf_op jit(solution)/shard_map/psum | solution.py:72
  (164 shorter events, 98.0 us)
Async XLA Ops:
  7.2 69.2 %all-gather.5.cloned.1.call-start = ((), (), s32[]{:S(2)}) async-start(), calls=%async_computation.1 | async-start | bytes 3932160 | tf_op jit(solution)/shard_map/all_gather | solution.py:27
  9.9 130.1 %all-gather.3.cloned.1.call-start = ((), (), s32[]{:S(2)}) async-start(), calls=%async_computation | async-start | bytes 3932160 | tf_op jit(solution)/shard_map/all_gather | solution.py:27
  10.6 305.7 %all-reduce.3.cloned.1.call-start = ((), (), s32[]{:S(2)}) async-start(), calls=%async_computation.2 | async-start | bytes 25165824 | tf_op jit(solution)/shard_map/psum | solution.py:13
  146.3 170.1 %copy-start.1 = (f32[1536,512]{1,0:T(8,128)S(1)}, f32[1536,512]{1,0:T(8,128)}, u32[]{:S(2)}) copy-start(f32[1536,512]{1,0:T(8,128)} %all-gather.3.cloned.1.call-done) | copy-start | bytes 9437188
  165.0 185.9 %copy-start.2 = (f32[1536]{0:T(1024)S(1)}, f32[1536]{0:T(1024)}, u32[]{:S(2)}) copy-start(f32[1536]{0:T(1024)} %param.5) | copy-start | bytes 18436
  390.2 6.5 copy-start
Sparse Core Ops, SparseCore 0:
  10.1 66.1 all-gather.4
  77.9 62.0 all-gather.2
  145.7 170.6 all-reduce.2
where the time goes:
time: 974 us; the launch traced here: 966 us
  blocking collectives  352 us (36%)
  waiting for transfers between devices  276 us (28%)
  matrix products  208 us (21%)
  local copies, waits for them, and re-layouts  63.6 us (7%)
  between operations  35.8 us (4%)
  other arithmetic  30 us (3%)
    psum x8, blocking collectives, shards(): image = lax.psum(placed, ('row', 'col'))  323 us
    psum x1, waiting for transfers between devices, from_root(): return lax.psum(jnp.where(mine, value, jnp.zeros_like(value)), axis)  151 us
    all_gather x2, waiting for transfers between devices, shards(): left_rows = lax.all_gather(piece, 'col', axis=0, tiled=True)  124 us
    dot_general x8, matrix products, shards(): partial_rows = jnp.dot(casida, unit_cols, precision=lax.Precision.HIGHEST)  103 us
    dot_general x2, matrix products, shards(): lax.dot_general(left_rows, right_rows, (((1,), (1,)), ((), ())), precisio...  73.9 us
    unnamed x8, local copies, waits for them, and re-layouts  43.9 us
  transfers between devices with their start and end apart: 3, of which 3 were waited for; matrix products, arithmetic and copies ran while one was open for 3% of the time, Pallas kernels for 0%

commit v1 on v0

--- a/solution.py
+++ b/solution.py
@@ -69,7 +69,7 @@
         placed = lax.dynamic_update_slice_in_dim(
             jnp.zeros((total_rows,), jnp.float32), partial_rows, row_index * rows_here, 0
         )
-        image = lax.psum(placed, ("row", "col"))
+        image = lax.psum(lax.psum(placed, "col"), "row")
         image = image - jnp.dot(
             upper_full,
             jnp.dot(lower_full.T, unit, precision=lax.Precision.HIGHEST),

time: 974 us -> 970 us (level)
    psum x8 -> x16, blocking collectives: 323 us -> 320 us  [shards(): image = lax.psum(lax.psum(placed, 'col'), 'row')]
where the time goes in v1:
time: 970 us; the launch traced here: 963 us
  blocking collectives  349 us (36%)
  waiting for transfers between devices  276 us (28%)
  matrix products  208 us (21%)
  local copies, waits for them, and re-layouts  63.6 us (7%)
  between operations  35.9 us (4%)
  other arithmetic  30 us (3%)
    psum x16, blocking collectives, shards(): image = lax.psum(lax.psum(placed, 'col'), 'row')  320 us
    psum x1, waiting for transfers between devices, from_root(): return lax.psum(jnp.where(mine, value, jnp.zeros_like(value)), axis)  151 us
    all_gather x2, waiting for transfers between devices, shards(): left_rows = lax.all_gather(piece, 'col', axis=0, tiled=True)  124 us
    dot_general x8, matrix products, shards(): partial_rows = jnp.dot(casida, unit_cols, precision=lax.Precision.HIGHEST)  103 us
    dot_general x2, matrix products, shards(): lax.dot_general(left_rows, right_rows, (((1,), (1,)), ((), ())), precisio...  73.9 us
    unnamed x8, local copies, waits for them, and re-layouts  43.9 us
    psum x1, blocking collectives, from_root(): return lax.psum(jnp.where(mine, value, jnp.zeros_like(value)), axis)  19.5 us
  transfers between devices with their start and end apart: 3, of which 3 were waited for; matrix products, arithmetic and copies ran while one was open for 3% of the time, Pallas kernels for 0%

profile of v1, /device:TPU:0, one launch (start us, length us, event | category | flops | bytes accessed | tf_op | source)
XLA Modules:
  0.0 962.5 jit_solution(18039939259899225421)
XLA Ops:
  10.7 65.6 %all-gather.5.cloned.1.call-done = f32[1536,512]{1,0:T(8,128)} async-done(((f32[384,512]{1,0:T(8,128)}), f32[1536,512]{1,0:T(8,128)}) %all-gather.5.cloned.1.call-update) | async-done | bytes 3145744 | tf_op jit(solution)/shard_map/all_gather | solution.py:27
  81.9 58.1 %all-gather.3.cloned.1.call-done = f32[1536,512]{1,0:T(8,128)} async-done(((f32[384,512]{1,0:T(8,128)}), f32[1536,512]{1,0:T(8,128)}) %all-gather.3.cloned.1.call-update) | async-done | bytes 3145744 | tf_op jit(solution)/shard_map/all_gather | solution.py:27
  146.3 18.8 %copy.9 = f32[1536,3072]{0,1:T(8,128)} copy(f32[1536,3072]{1,0:T(8,128)} %param.4) | data formatting | bytes 37748736 | tf_op args[1]
  165.1 151.2 %all-reduce.3.cloned.1.call-done = (f32[1536,512]{1,0:T(8,128)}, f32[1536,512]{1,0:T(8,128)}, f32[1536,512]{1,0:T(8,128)}, f32[1536,512]{1,0:T(8,128)}) async-done(((f32[1536,512]{1,0:T(8,128)}, f32[1536,512]{1,0:T(8,128)}, f32[1536,512]{1,0:T(8,128)}, f32[1536,512]{1,0:T(8,128)}), (f32[1536,512]{1,0:T(8,128)}, f32[1536,512]{1,0:T(8,128)}, f32[1536,512]{1,0:T(8,128)}, ...) | async-done | bytes 12582928 | tf_op jit(solution)/shard_map/psum | solution.py:13
  316.4 34.6 %fusion.2 = f32[3072,1536]{1,0:T(8,128)} fusion(f32[1536,512]{1,0:T(8,128)S(1)} %copy-done.1, f32[1536,512]{1,0:T(8,128)} %get-tuple-element.12, f32[1536,512]{1,0:T(8,128)} %get-tuple-element.13), kind=kOutput, calls=%fused_computation.3 | convolution fusion | flops 28992602112 | bytes 28311552 | tf_op jit(solution)/shard_map/dot_general | solution.py:32
  351.0 39.2 %fusion.1 = f32[1536,3072]{0,1:T(8,128)S(1)} fusion(f32[1536,3072]{0,1:T(8,128)} %copy.9, f32[3072,1536]{1,0:T(8,128)} %fusion.2, f32[1536,512]{1,0:T(8,128)} %all-gather.5.cloned.1.call-done, f32[1536]{0:T(1024)S(1)} %copy-done.2, s32[1536]{0:T(1024)S(1)} %iota_add_fusion.1, s32[3072]{0:T(1024)S(1)} %iota_add_fusion, f32[1536,512]{1,0:T(8,128)} %get-tuple-element.14, ...), kind=kOutput, calls=%fused_computation.2 | convolution fusion | flops 29020913664 | bytes 66084864 | tf_op jit(solution)/shard_map/dot_general | solution.py:32
  396.7 19.5 %psum.151 = f32[1536,8]{0,1:T(8,128)S(1)} all-reduce(f32[1536,8]{0,1:T(8,128)S(1)} %slice_select_fusion), channel_id=1, replica_groups=mesh['row'=8,'col'=4] {'col'}, use_global_device_ids=true, to_apply=%region_4.5 | all-reduce | flops 12288 | bytes 98304 | tf_op jit(solution)/shard_map/psum | solution.py:13
  443.8 16.1 %psum.152 = f32[12288]{0:T(1024)S(1)} all-reduce(f32[12288]{0:T(1024)S(1)} %dynamic_update_slice.24), channel_id=1, replica_groups=mesh['row'=8,'col'=4] {'col'}, use_global_device_ids=true, to_apply=%region_6.7 | all-reduce | flops 12288 | bytes 98304 | tf_op jit(solution)/shard_map/psum | solution.py:72
  459.9 22.9 %psum.153 = f32[12288]{0:T(1024)S(1)} all-reduce(f32[12288]{0:T(1024)S(1)} %psum.152), channel_id=1, replica_groups=mesh['row'=8,'col'=4] {'row'}, use_global_device_ids=true, to_apply=%region_7.8 | all-reduce | flops 12288 | bytes 98304 | tf_op jit(solution)/shard_map/psum | solution.py:72
  507.6 17.9 %psum.154 = f32[12288]{0:T(1024)S(1)} all-reduce(f32[12288]{0:T(1024)S(1)} %dynamic_update_slice.25), channel_id=1, replica_groups=mesh['row'=8,'col'=4] {'col'}, use_global_device_ids=true, to_apply=%region_10.11 | all-reduce | flops 12288 | bytes 98304 | tf_op jit(solution)/shard_map/psum | solution.py:72
  525.5 23.0 %psum.155 = f32[12288]{0:T(1024)S(1)} all-reduce(f32[12288]{0:T(1024)S(1)} %psum.154), channel_id=1, replica_groups=mesh['row'=8,'col'=4] {'row'}, use_global_device_ids=true, to_apply=%region_11.12 | all-reduce | flops 12288 | bytes 98304 | tf_op jit(solution)/shard_map/psum | solution.py:72
  571.7 16.1 %psum.156 = f32[12288]{0:T(1024)S(1)} all-reduce(f32[12288]{0:T(1024)S(1)} %dynamic_update_slice.26), channel_id=1, replica_groups=mesh['row'=8,'col'=4] {'col'}, use_global_device_ids=true, to_apply=%region_14.15 | all-reduce | flops 12288 | bytes 98304 | tf_op jit(solution)/shard_map/psum | solution.py:72
  587.9 23.0 %psum.157 = f32[12288]{0:T(1024)S(1)} all-reduce(f32[12288]{0:T(1024)S(1)} %psum.156), channel_id=1, replica_groups=mesh['row'=8,'col'=4] {'row'}, use_global_device_ids=true, to_apply=%region_15.16 | all-reduce | flops 12288 | bytes 98304 | tf_op jit(solution)/shard_map/psum | solution.py:72
  634.3 17.8 %psum.158 = f32[12288]{0:T(1024)S(1)} all-reduce(f32[12288]{0:T(1024)S(1)} %dynamic_update_slice.27), channel_id=1, replica_groups=mesh['row'=8,'col'=4] {'col'}, use_global_device_ids=true, to_apply=%region_18.19 | all-reduce | flops 12288 | bytes 98304 | tf_op jit(solution)/shard_map/psum | solution.py:72
  652.1 23.3 %psum.159 = f32[12288]{0:T(1024)S(1)} all-reduce(f32[12288]{0:T(1024)S(1)} %psum.158), channel_id=1, replica_groups=mesh['row'=8,'col'=4] {'row'}, use_global_device_ids=true, to_apply=%region_19.20 | all-reduce | flops 12288 | bytes 98304 | tf_op jit(solution)/shard_map/psum | solution.py:72
  699.0 16.2 %psum.160 = f32[12288]{0:T(1024)S(1)} all-reduce(f32[12288]{0:T(1024)S(1)} %dynamic_update_slice.28), channel_id=1, replica_groups=mesh['row'=8,'col'=4] {'col'}, use_global_device_ids=true, to_apply=%region_22.23 | all-reduce | flops 12288 | bytes 98304 | tf_op jit(solution)/shard_map/psum | solution.py:72
  715.2 23.0 %psum.161 = f32[12288]{0:T(1024)S(1)} all-reduce(f32[12288]{0:T(1024)S(1)} %psum.160), channel_id=1, replica_groups=mesh['row'=8,'col'=4] {'row'}, use_global_device_ids=true, to_apply=%region_23.24 | all-reduce | flops 12288 | bytes 98304 | tf_op jit(solution)/shard_map/psum | solution.py:72
  761.7 17.8 %psum.162 = f32[12288]{0:T(1024)S(1)} all-reduce(f32[12288]{0:T(1024)S(1)} %dynamic_update_slice.29), channel_id=1, replica_groups=mesh['row'=8,'col'=4] {'col'}, use_global_device_ids=true, to_apply=%region_26.27 | all-reduce | flops 12288 | bytes 98304 | tf_op jit(solution)/shard_map/psum | solution.py:72
  779.6 23.0 %psum.163 = f32[12288]{0:T(1024)S(1)} all-reduce(f32[12288]{0:T(1024)S(1)} %psum.162), channel_id=1, replica_groups=mesh['row'=8,'col'=4] {'row'}, use_global_device_ids=true, to_apply=%region_27.28 | all-reduce | flops 12288 | bytes 98304 | tf_op jit(solution)/shard_map/psum | solution.py:72
  825.8 16.3 %psum.164 = f32[12288]{0:T(1024)S(1)} all-reduce(f32[12288]{0:T(1024)S(1)} %dynamic_update_slice.30), channel_id=1, replica_groups=mesh['row'=8,'col'=4] {'col'}, use_global_device_ids=true, to_apply=%region_30.31 | all-reduce | flops 12288 | bytes 98304 | tf_op jit(solution)/shard_map/psum | solution.py:72
  842.1 23.0 %psum.165 = f32[12288]{0:T(1024)S(1)} all-reduce(f32[12288]{0:T(1024)S(1)} %psum.164), channel_id=1, replica_groups=mesh['row'=8,'col'=4] {'row'}, use_global_device_ids=true, to_apply=%region_31.32 | all-reduce | flops 12288 | bytes 98304 | tf_op jit(solution)/shard_map/psum | solution.py:72
  874.5 18.6 %copy.10 = f32[1536,3072]{1,0:T(8,128)} copy(f32[1536,3072]{0,1:T(8,128)} %copy-done) | data formatting | bytes 37748736
  906.8 17.7 %psum.166 = f32[12288]{0:T(1024)S(1)} all-reduce(f32[12288]{0:T(1024)S(1)} %dynamic_update_slice.31), channel_id=1, replica_groups=mesh['row'=8,'col'=4] {'col'}, use_global_device_ids=true, to_apply=%region_34.35 | all-reduce | flops 12288 | bytes 98304 | tf_op jit(solution)/shard_map/psum | solution.py:72
  924.5 22.8 %psum.167 = f32[12288]{0:T(1024)S(1)} all-reduce(f32[12288]{0:T(1024)S(1)} %psum.166), channel_id=1, replica_groups=mesh['row'=8,'col'=4] {'row'}, use_global_device_ids=true, to_apply=%region_35.36 | all-reduce | flops 12288 | bytes 98304 | tf_op jit(solution)/shard_map/psum | solution.py:72
  (172 shorter events, 200.9 us)
Async XLA Ops:
  7.2 69.2 %all-gather.5.cloned.1.call-start = ((), (), s32[]{:S(2)}) async-start(), calls=%async_computation.1 | async-start | bytes 3932160 | tf_op jit(solution)/shard_map/all_gather | solution.py:27
  9.9 130.1 %all-gather.3.cloned.1.call-start = ((), (), s32[]{:S(2)}) async-start(), calls=%async_computation | async-start | bytes 3932160 | tf_op jit(solution)/shard_map/all_gather | solution.py:27
  10.6 305.7 %all-reduce.3.cloned.1.call-start = ((), (), s32[]{:S(2)}) async-start(), calls=%async_computation.2 | async-start | bytes 25165824 | tf_op jit(solution)/shard_map/psum | solution.py:13
  146.3 170.1 %copy-start.1 = (f32[1536,512]{1,0:T(8,128)S(1)}, f32[1536,512]{1,0:T(8,128)}, u32[]{:S(2)}) copy-start(f32[1536,512]{1,0:T(8,128)} %all-gather.3.cloned.1.call-done) | copy-start | bytes 9437188
  165.0 185.9 %copy-start.2 = (f32[1536]{0:T(1024)S(1)}, f32[1536]{0:T(1024)}, u32[]{:S(2)}) copy-start(f32[1536]{0:T(1024)} %param.5) | copy-start | bytes 18436
  390.2 6.5 copy-start
Sparse Core Ops, SparseCore 0:
  10.1 66.1 all-gather.4
  77.9 62.0 all-gather.2
  145.7 170.6 all-reduce.2
